TPU v7x, 32 devices: a whole 2x2x4 slice. The times are simulated.
32 devices in a mesh: gx: 8 (over z, x), gy: 4 (over y, core).
Axes of the slice: x: 2, y: 2, z: 4, core: 2. Of those that a mesh axis runs over, the one named last changes fastest.
Arguments:
- species: float32 [53, 32, 32, 128], P(None, 'gx', 'gy'), may hold values from -6 to 6
- diffusion: float32 [53], replicated, may hold values from 0.02 to 0.15
- class_rate: float32 [4], replicated, may hold values from 0.2 to 1
- mixing: float32 [53, 53], replicated, may hold values from -0.3 to 0.3
- inverses: float32 [4, 53, 53], replicated, may hold values from -0.01 to 0.12
- newton_counts: int32 [4], replicated, may hold values from 1 to 8, as said below
- cell_class: int32 [32, 32, 128], P('gx', 'gy'), may hold values from 0 to 3
Outputs:
- updated: float32 [53, 32, 32, 128], P(None, 'gx', 'gy')
Inputs may be any that keep to these rules, and one draw needn't show every extreme that they name: `newton_counts`: nondecreasing in the class; the last class takes 8.
All inputs are finite; a program needn't handle non-finite values.
Results may differ from a plain program's by a relative error of at most 0.0003.
Values sent between devices are 32-bit elements; how exact they have to be, the bound alone decides.
A program may use at most 64 MiB of HBM per device.

v0:
```python
import functools

import jax
import jax.numpy as jnp
from jax import lax
from jax.experimental import pallas as pl
from jax.experimental.pallas import tpu as pltpu
from jax.sharding import PartitionSpec as P

NMAX = 8
CHUNK = 2
GROUP = 1
SPAN = 4
UNROLL = 8
MESH = pl.DeviceIdType.MESH
F32 = jnp.float32
BF16 = jnp.bfloat16


def kernel(
    dims,
    species_hbm, diffusion_ref, rate_ref, mixing_ref, inverses_ref, counts_ref, class_ref,
    out_ref,
    raw, ext, ext2, forcing, target, coef, square, mix_w, inv_w,
    load_sem, xs_send, xs_recv, ys_send, ys_recv,
):
    spec, nx, ny, nz, nclass = dims
    rows = nx * ny
    pad = ext.shape[2]
    chunks = ny // CHUNK
    gx, gy = lax.axis_index("gx"), lax.axis_index("gy")
    sx, sy = lax.axis_size("gx"), lax.axis_size("gy")
    has_x = (gx > 0, gx < sx - 1)
    has_y = (gy > 0, gy < sy - 1)
    to_x = ((gx - 1, gy), (gx + 1, gy))
    to_y = ((gx, gy - 1), (gx, gy + 1))

    load = pltpu.make_async_copy(species_hbm, raw, load_sem)
    load.start()

    zero_col = jnp.zeros((pad, nz), F32)
    for buf in (ext, ext2):
        for y in range(ny):
            buf[0, y + 1] = zero_col
            buf[nx + 1, y + 1] = zero_col
        for x in range(nx):
            buf[x + 1, 0] = zero_col
            buf[x + 1, ny + 1] = zero_col

    barrier = pltpu.get_barrier_semaphore()
    for has, to in zip(has_x + has_y, to_x + to_y):
        @pl.when(has)
        def _():
            pl.semaphore_signal(barrier, inc=1, device_id=to, device_id_type=MESH)

    def x_copy(stage, side, c):
        buf = (ext, ext2)[stage]
        src_row, dst_row = (1, nx + 1) if side == 0 else (nx, 0)
        ys = pl.ds(1 + c * CHUNK, CHUNK)
        return pltpu.make_async_remote_copy(
            src_ref=buf.at[src_row, ys, pl.ds(0, spec)], dst_ref=buf.at[dst_row, ys, pl.ds(0, spec)],
            send_sem=xs_send.at[stage, side, c], recv_sem=xs_recv.at[stage, side, c],
            device_id=to_x[side], device_id_type=MESH)

    def y_copy(stage, side):
        buf = (ext, ext2)[stage]
        src_col, dst_col = (1, ny + 1) if side == 0 else (ny, 0)
        return pltpu.make_async_remote_copy(
            src_ref=buf.at[pl.ds(1, nx), src_col, pl.ds(0, spec)],
            dst_ref=buf.at[pl.ds(1, nx), dst_col, pl.ds(0, spec)],
            send_sem=ys_send.at[stage, side], recv_sem=ys_recv.at[stage, side],
            device_id=to_y[side], device_id_type=MESH)

    def x_arrive(stage, c):
        for side in (0, 1):
            @pl.when(has_x[side])
            def _():
                x_copy(stage, 1 - side, c).wait_recv()

    def y_arrive(stage):
        for side in (0, 1):
            @pl.when(has_y[side])
            def _():
                y_copy(stage, 1 - side).wait_recv()

    load.wait()

    def relay(x):
        for y in range(ny):
            col = raw[pl.ds(x * ny + y, spec, stride=rows), :]
            ext[x + 1, y + 1] = jnp.concatenate([col, jnp.zeros((pad - spec, nz), F32)], axis=0)

    relay(0)
    relay(nx - 1)
    neighbours = sum(has.astype(jnp.int32) for has in has_x + has_y)
    pl.semaphore_wait(barrier, neighbours)
    for c in range(chunks):
        for side in (0, 1):
            @pl.when(has_x[side])
            def _():
                x_copy(0, side, c).start()
    for x in range(1, nx - 1):
        relay(x)
    for side in (0, 1):
        @pl.when(has_y[side])
        def _():
            y_copy(0, side).start()

    square[...] = jnp.zeros_like(square)

    def split_weight(value):
        square[0:spec, 0:spec] = value
        w = square[...]
        high = w.astype(BF16).astype(F32)
        both = high + pltpu.roll((w - high).astype(BF16).astype(F32), 64, 1)
        return jnp.concatenate([both, both], axis=1)[:, :192]

    mix_w[...] = split_weight(mixing_ref[...]).astype(BF16)
    inv_w[...] = jnp.concatenate(
        [split_weight(inverses_ref[:, k, :])[:pad] for k in range(nclass)], axis=0).astype(BF16)
    square[...] = jnp.zeros_like(square)
    square[0:1, 0:spec] = diffusion_ref[...]
    line = jnp.broadcast_to(square[0:1, :], square.shape)
    on = lax.broadcasted_iota(jnp.int32, square.shape, 0) == lax.broadcasted_iota(
        jnp.int32, square.shape, 1)
    column = jnp.sum(jnp.where(on, line, 0.0), axis=1, keepdims=True)
    coef[...] = jnp.broadcast_to(column[:pad], coef.shape)

    lane = lax.broadcasted_iota(jnp.int32, (pad, nz), 1)

    def laplace(buf, x, y):
        v = buf[x + 1, y + 1]
        total = buf[x + 2, y + 1] + buf[x, y + 1] + buf[x + 1, y + 2] + buf[x + 1, y]
        total = total + jnp.where(lane == nz - 1, 0.0, pltpu.roll(v, nz - 1, 1))
        total = total + jnp.where(lane == 0, 0.0, pltpu.roll(v, 1, 1))
        return v, total - 6.0 * v

    def split_rows(v):
        v = jnp.concatenate([v, jnp.zeros((64 - pad, v.shape[1]), F32)], axis=0)
        high = v.astype(BF16)
        low = (v - high.astype(F32)).astype(BF16)
        return jnp.concatenate([high, high, low], axis=0)

    def solve(xs, first):
        groups = [[(x, first + g * GROUP + j) for x in xs for j in range(GROUP)]
                  for g in range(SPAN // GROUP)]
        starts, rates, whiches, limits = [], [], [], []
        for g, cells in enumerate(groups):
            parts = []
            for x, y in cells:
                v, lap = laplace(ext, x, y)
                force = coef[...] * lap
                forcing[x, y] = force
                parts.append(v + force)
            start = jnp.concatenate(parts, axis=1)
            target[g] = start
            which = jnp.concatenate([class_ref[pl.ds(x * ny + y, 1), :] for x, y in cells], axis=1)
            cell_rate = jnp.zeros(which.shape, F32)
            cell_count = jnp.zeros(which.shape, jnp.int32)
            for k in range(nclass):
                cell_rate = jnp.where(which == k, rate_ref[k], cell_rate)
                cell_count = jnp.where(which == k, counts_ref[k], cell_count)
            starts.append(start)
            rates.append(cell_rate)
            whiches.append(which)
            limits.append(cell_count)

        def step(k, ys):
            out = []
            for g, y in enumerate(ys):
                product = jnp.dot(mix_w[...], split_rows(jnp.tanh(y)), preferred_element_type=F32)[:pad]
                residual = y - target[g] - rates[g] * (product - y)
                fixes = jnp.dot(inv_w[...], split_rows(residual), preferred_element_type=F32)
                active = jnp.where(k < limits[g], whiches[g], nclass)
                fix = jnp.zeros_like(y)
                for n in range(nclass):
                    fix = jnp.where(active == n, fixes[n * pad:(n + 1) * pad], fix)
                out.append(y - fix)
            return tuple(out)

        values = lax.fori_loop(0, NMAX, step, tuple(starts), unroll=UNROLL)
        for cells, value in zip(groups, values):
            for i, (x, y) in enumerate(cells):
                ext2[x + 1, y + 1] = value[:, i * nz:(i + 1) * nz]

    y_arrive(0)

    def inner(c, carry):
        solve(tuple(range(1, nx - 1)), c * SPAN)
        return carry

    def outer(c, carry):
        per = SPAN // CHUNK
        for i in range(per):
            x_arrive(0, c * per + i)
        solve((0, nx - 1), c * SPAN)
        for side in (0, 1):
            @pl.when(has_x[side])
            def _():
                for i in range(per):
                    x_copy(1, side, c * per + i).start()
        return carry

    spans = ny // SPAN
    early = (spans + 1) // 2
    if nx > 2:
        lax.fori_loop(0, early, inner, 0)
    lax.fori_loop(0, spans, outer, 0)
    if nx > 2:
        lax.fori_loop(early, spans, inner, 0)
    for side in (0, 1):
        @pl.when(has_y[side])
        def _():
            y_copy(1, side).start()

    def finish(x, y):
        v, lap = laplace(ext2, x, y)
        new = v + 0.5 * (coef[...] * lap - forcing[x, y])
        out_ref[pl.ds(x * ny + y, spec, stride=rows), :] = new[:spec]

    for x in range(1, nx - 1):
        for y in range(1, ny - 1):
            finish(x, y)
    y_arrive(1)
    for x in range(1, nx - 1):
        finish(x, 0)
        finish(x, ny - 1)

    def last(c, carry):
        x_arrive(1, c)
        for j in range(CHUNK):
            for x in (0, nx - 1):
                finish(x, c * CHUNK + j)
        return carry

    lax.fori_loop(0, chunks, last, 0)

    for stage in (0, 1):
        for side in (0, 1):
            @pl.when(has_x[side])
            def _():
                for c in range(chunks):
                    x_copy(stage, side, c).wait_send()
            @pl.when(has_y[side])
            def _():
                y_copy(stage, side).wait_send()


def local(species, diffusion, class_rate, mixing, inverses, newton_counts, cell_class):
    spec, nx, ny, nz = species.shape
    nclass = inverses.shape[0]
    pad = -(-spec // 8) * 8
    chunks = ny // CHUNK
    width = 2 * GROUP * nz
    vmem = pl.BlockSpec(memory_space=pltpu.VMEM)
    smem = pl.BlockSpec(memory_space=pltpu.SMEM)
    out = pl.pallas_call(
        functools.partial(kernel, (spec, nx, ny, nz, nclass)),
        out_shape=pltpu.VMEM((spec * nx * ny, nz), F32),
        in_specs=[pl.BlockSpec(memory_space=pl.ANY), vmem, smem, vmem, vmem, smem, vmem],
        out_specs=vmem,
        scratch_shapes=[
            pltpu.VMEM((spec * nx * ny, nz), F32),
            pltpu.VMEM((nx + 2, ny + 2, pad, nz), F32),
            pltpu.VMEM((nx + 2, ny + 2, pad, nz), F32),
            pltpu.VMEM((nx, ny, pad, nz), F32),
            pltpu.VMEM((SPAN // GROUP, pad, width), F32),
            pltpu.VMEM((pad, nz), F32),
            pltpu.VMEM((64, 128), F32),
            pltpu.VMEM((64, 192), BF16),
            pltpu.VMEM((nclass * pad, 192), BF16),
            pltpu.SemaphoreType.DMA(()),
            pltpu.SemaphoreType.DMA((2, 2, chunks)),
            pltpu.SemaphoreType.DMA((2, 2, chunks)),
            pltpu.SemaphoreType.DMA((2, 2)),
            pltpu.SemaphoreType.DMA((2, 2)),
        ],
        compiler_params=pltpu.CompilerParams(
            collective_id=0, has_side_effects=True, vmem_limit_bytes=60 * 1024 * 1024),
    )(
        species.reshape(spec * nx * ny, nz), diffusion.reshape(1, spec), class_rate,
        mixing, inverses.transpose(1, 0, 2), newton_counts, cell_class.reshape(nx * ny, nz),
    )
    return out.reshape(species.shape)


def solution(mesh):
    in_specs = (P(None, "gx", "gy", None), P(), P(), P(), P(), P(), P("gx", "gy", None))
    out_specs = P(None, "gx", "gy", None)
    return jax.shard_map(local, mesh=mesh, in_specs=in_specs, out_specs=out_specs, check_vma=False)
```

profile of v0, /device:TPU:3, one launch (start us, length us, event | category | flops | bytes accessed | tf_op | source)
XLA Modules:
  0.0 30.2 jit_solution(7063981935735111660)
XLA Ops:
  0.0 29.2 %shard_map.73 = f32[1696,128]{1,0:T(8,128)S(1)} custom-call(f32[1696,128]{1,0:T(8,128)} %bitcast.6, f32[1,53]{1,0:T(1,128)} %bitcast.9, f32[4]{0:T(128)} %rate_ref.1, f32[53,53]{1,0:T(8,128)} %mixing_ref.1, f32[53,4,53]{2,1,0:T(4,128)} %bitcast.7, s32[4]{0:T(128)} %counts_ref.1, s32[32,128]{1,0:T(8,128)} %bitcast.8), custom_call_target="tpu_custom_call" | custom-call | tf_op jit(solution)/shard_map/pallas_call | solution.py:257
  29.2 0.9 %copy.9 = f32[53,4,8,128]{3,2,1,0:T(8,128)} copy(f32[53,4,8,128]{3,2,1,0:T(8,128)S(1)} %bitcast.5) | data formatting | bytes 1736704
where the time goes:
time: 30.3 us; the launch traced here: 30.2 us
  Pallas kernels  29.2 us (96%)
  local copies, waits for them, and re-layouts  0.91 us (3%)
    pallas_call x1, Pallas kernels, local(): pl.pallas_call(functools.partial(kernel, (spec, nx, ny, nz, nclass)), out...  29.2 us
    unnamed x1, local copies, waits for them, and re-layouts  0.91 us

commit v1 on v0

v1 whole, which is shorter than its diff:
```python
import functools

import jax
import jax.numpy as jnp
from jax import lax
from jax.experimental import pallas as pl
from jax.experimental.pallas import tpu as pltpu
from jax.sharding import PartitionSpec as P

NMAX = 8
SPAN = 4
MESH = pl.DeviceIdType.MESH
F32 = jnp.float32
BF16 = jnp.bfloat16


def pairs_of(n):
    return [tuple(sorted({c, n - 1 - c})) for c in range((n + 1) // 2)]


def kernel(
    dims,
    species_hbm, diffusion_hbm, rate_hbm, mixing_hbm, inverses_hbm, counts_hbm, class_hbm,
    out,
    ext, ext2, scaled, coef, row, mix, inv, stack, square, w_high, w_low, classes, rates, counts,
    load_sem, small_sem, xs_send, xs_recv, ys_send, ys_recv,
):
    spec, nx, ny, nz, nclass = dims
    pad = ext.shape[2]
    real = pl.ds(0, spec)
    gx, gy = lax.axis_index("gx"), lax.axis_index("gy")
    sx, sy = lax.axis_size("gx"), lax.axis_size("gy")
    has_x = (gx > 0, gx < sx - 1)
    has_y = (gy > 0, gy < sy - 1)
    to_x = ((gx - 1, gy), (gx + 1, gy))
    to_y = ((gx, gy - 1), (gx, gy + 1))
    edges = pairs_of(ny)

    def load(x, y):
        return pltpu.make_async_copy(
            species_hbm.at[:, x, y], ext.at[x + 1, y + 1, real], load_sem.at[x, y])

    sides = sorted({0, nx - 1})
    first = [(x, y) for y in edges[0] for x in sides]
    first += [(x, y) for y in edges[0] for x in range(1, nx - 1)]
    first += [(x, y) for pair in edges[1:] for y in pair for x in sides]
    later = [(x, y) for pair in edges[1:] for y in pair for x in range(1, nx - 1)]
    for x, y in first + later:
        load(x, y).start()
    small = [
        pltpu.make_async_copy(src, dst, small_sem.at[i]) for i, (src, dst) in enumerate((
            (mixing_hbm, mix), (inverses_hbm, inv), (diffusion_hbm, row),
            (rate_hbm, rates), (counts_hbm, counts), (class_hbm, classes)))]
    for copy in small:
        copy.start()

    barrier = pltpu.get_barrier_semaphore()
    for has, to in zip(has_x + has_y, to_x + to_y):
        @pl.when(has)
        def _():
            pl.semaphore_signal(barrier, inc=1, device_id=to, device_id_type=MESH)

    tail = jnp.zeros((pad - spec, nz), F32)
    for x in range(nx + 2):
        for y in range(ny + 2):
            halo = x in (0, nx + 1) or y in (0, ny + 1)
            if x in (0, nx + 1) and y in (0, ny + 1):
                continue
            ext[x, y, pl.ds(spec, pad - spec)] = tail
            if halo:
                ext2[x, y, pl.ds(spec, pad - spec)] = tail
    blank = jnp.zeros((spec, nz), F32)
    for side in (0, 1):
        @pl.when(jnp.logical_not(has_x[side]))
        def _():
            for buf in (ext, ext2):
                for y in range(ny):
                    buf[side * (nx + 1), y + 1, real] = blank
        @pl.when(jnp.logical_not(has_y[side]))
        def _():
            for buf in (ext, ext2):
                for x in range(nx):
                    buf[x + 1, side * (ny + 1), real] = blank

    def x_copy(stage, side, y):
        buf = (ext, ext2)[stage]
        src_row, dst_row = (1, nx + 1) if side == 0 else (nx, 0)
        return pltpu.make_async_remote_copy(
            src_ref=buf.at[src_row, y + 1, real], dst_ref=buf.at[dst_row, y + 1, real],
            send_sem=xs_send.at[stage, side, y], recv_sem=xs_recv.at[stage, side, y],
            device_id=to_x[side], device_id_type=MESH)

    def y_copy(stage, side):
        buf = (ext, ext2)[stage]
        src_col, dst_col = (1, ny + 1) if side == 0 else (ny, 0)
        return pltpu.make_async_remote_copy(
            src_ref=buf.at[pl.ds(1, nx), src_col, real],
            dst_ref=buf.at[pl.ds(1, nx), dst_col, real],
            send_sem=ys_send.at[stage, side], recv_sem=ys_recv.at[stage, side],
            device_id=to_y[side], device_id_type=MESH)

    def x_start(stage, ys):
        for side in (0, 1):
            @pl.when(has_x[side])
            def _():
                for y in ys:
                    x_copy(stage, side, y).start()

    def x_arrive(stage, ys):
        for side in (0, 1):
            @pl.when(has_x[side])
            def _():
                for y in ys:
                    x_copy(stage, 1 - side, y).wait_recv()

    def y_start(stage):
        for side in (0, 1):
            @pl.when(has_y[side])
            def _():
                y_copy(stage, side).start()

    def y_arrive(stage):
        for side in (0, 1):
            @pl.when(has_y[side])
            def _():
                y_copy(stage, 1 - side).wait_recv()

    neighbours = sum(has.astype(jnp.int32) for has in has_x + has_y)
    pl.semaphore_wait(barrier, neighbours)
    for x, y in first:
        load(x, y).wait()
    x_start(0, edges[0])
    y_start(0)
    for pair in edges[1:]:
        x_start(0, pair)

    for copy in small:
        copy.wait()
    stack[...] = jnp.zeros_like(stack)
    square[...] = jnp.zeros_like(square)
    square[0:1, 0:spec] = row[...]
    line = jnp.broadcast_to(square[0:1, :], square.shape)
    on = lax.broadcasted_iota(jnp.int32, square.shape, 0) == lax.broadcasted_iota(
        jnp.int32, square.shape, 1)
    column = jnp.sum(jnp.where(on, line, 0.0), axis=1, keepdims=True)
    coef[...] = jnp.broadcast_to(column[:pad], coef.shape)
    square[0:spec, 0:spec] = mix[...]
    for k in range(nclass):
        stack[k * pad:k * pad + spec, 0:spec] = inv[:, k, :]
    mixed = jnp.dot(
        stack[...], square[...], precision=lax.Precision.HIGHEST, preferred_element_type=F32)
    spread = lax.broadcasted_iota(jnp.int32, (pad, 128), 1)
    highs, lows = [], []
    for k in range(nclass):
        rate = rates[k]
        own = stack[k * pad:(k + 1) * pad, :] * -(1.0 + rate)
        other = mixed[k * pad:(k + 1) * pad, :] * (rate * (1.0 + rate))
        both = own + pltpu.roll(other, pad, 1)
        high = both.astype(BF16).astype(F32)
        for part, into in ((high, highs), (both - high, lows)):
            turned = pltpu.roll(part, 2 * pad, 1)
            into.append(jnp.concatenate(
                [jnp.where(spread < 2 * pad, part, turned), turned], axis=1))
    for parts, ref in ((highs, w_high), (lows, w_low)):
        ref[...] = jnp.concatenate(
            [parts[k][t * 8:(t + 1) * 8] for t in range(pad // 8) for k in range(nclass)],
            axis=0)[:, :4 * pad].astype(BF16)

    lane = lax.broadcasted_iota(jnp.int32, (pad, nz), 1)

    def laplace(buf, x, y):
        v = buf[x + 1, y + 1]
        total = buf[x + 2, y + 1] + buf[x, y + 1] + buf[x + 1, y + 2] + buf[x + 1, y]
        total = total + jnp.where(lane == nz - 1, 0.0, pltpu.roll(v, nz - 1, 1))
        total = total + jnp.where(lane == 0, 0.0, pltpu.roll(v, 1, 1))
        return v, total - 6.0 * v

    def solve(groups):
        states, shrinks, whiches, limits = [], [], [], []
        for g, cells in enumerate(groups):
            parts = []
            for x, y in cells:
                v, lap = laplace(ext, x, y)
                force = coef[...] * lap
                out[x, y] = force
                parts.append(v + force)
            target = jnp.concatenate(parts, axis=1)
            which = jnp.concatenate([classes[pl.ds(x * ny + y, 1), :] for x, y in cells], axis=1)
            cell_rate = jnp.zeros(which.shape, F32)
            cell_count = jnp.zeros(which.shape, jnp.int32)
            for k in range(nclass):
                cell_rate = jnp.where(which == k, rates[k], cell_rate)
                cell_count = jnp.where(which == k, counts[k], cell_count)
            shrink = 1.0 / (1.0 + cell_rate)
            scaled[g, :, :target.shape[1]] = target * shrink
            states.append(target * cell_rate)
            shrinks.append(shrink)
            whiches.append(which)
            limits.append(cell_count)

        def value(g, state):
            return state * shrinks[g] + scaled[g, :, :state.shape[1]]

        def step(k, states):
            result = []
            for g, state in enumerate(states):
                z = jnp.concatenate([state, jnp.tanh(value(g, state))], axis=0)
                high = z.astype(BF16)
                low = (z - high.astype(F32)).astype(BF16)
                z = jnp.concatenate([high, low], axis=0)
                fixes = jnp.dot(w_high[...], z, preferred_element_type=F32)
                fixes = fixes + jnp.dot(w_low[...], z, preferred_element_type=F32)
                active = jnp.where(k < limits[g], whiches[g], nclass)
                picks = [active == n for n in range(nclass)]
                tiles = []
                for t in range(pad // 8):
                    fix = jnp.zeros((8, state.shape[1]), F32)
                    for n in range(nclass):
                        at = (t * nclass + n) * 8
                        fix = jnp.where(picks[n], fixes[at:at + 8], fix)
                    tiles.append(fix)
                result.append(state + jnp.concatenate(tiles, axis=0))
            return tuple(result)

        states = lax.fori_loop(0, NMAX, step, tuple(states), unroll=NMAX)
        for g, (cells, state) in enumerate(zip(groups, states)):
            end = value(g, state)
            for i, (x, y) in enumerate(cells):
                ext2[x + 1, y + 1] = end[:, i * nz:(i + 1) * nz]

    def pack(cells):
        return [cells[i:i + 2] for i in range(0, len(cells), 2)]

    def solve_all(cells):
        groups = pack(cells)
        for i in range(0, len(groups), SPAN):
            solve(groups[i:i + SPAN])

    for x, y in later:
        load(x, y).wait()
    middle = list(range(1, nx - 1))
    free = [(x, y) for pair in edges[1:] for y in pair for x in middle]
    rim = [(x, y) for y in edges[0] for x in middle]
    now = 2 * SPAN * (len(free) // (2 * SPAN))
    solve_all(free[:now])
    y_arrive(0)
    solve_all(free[now:] + rim)
    per = max(1, SPAN // 2)
    for c in range(0, len(edges), per):
        ys = [y for pair in edges[c:c + per] for y in pair]
        x_arrive(0, ys)
        solve_all([(x, y) for y in ys for x in sides])
        x_start(1, ys)
        if c == 0:
            y_start(1)

    def finish(x, y):
        v, lap = laplace(ext2, x, y)
        out[x, y] = v + 0.5 * (coef[...] * lap - out[x, y])

    for x, y in free:
        finish(x, y)
    y_arrive(1)
    for x, y in rim:
        finish(x, y)
    for pair in edges:
        x_arrive(1, pair)
        for y in pair:
            for x in sides:
                finish(x, y)

    for stage in (0, 1):
        for side in (0, 1):
            @pl.when(has_x[side])
            def _():
                for y in range(ny):
                    x_copy(stage, side, y).wait_send()
            @pl.when(has_y[side])
            def _():
                y_copy(stage, side).wait_send()


def deliver(held, out_hbm, sem):
    spec, nx, ny, _ = out_hbm.shape
    copies = [
        pltpu.make_async_copy(held.at[x, y, pl.ds(0, spec)], out_hbm.at[:, x, y], sem.at[x, y])
        for x in range(nx) for y in range(ny)]
    for copy in copies:
        copy.start()
    for copy in copies:
        copy.wait()


def local(species, diffusion, class_rate, mixing, inverses, newton_counts, cell_class):
    spec, nx, ny, nz = species.shape
    nclass = inverses.shape[0]
    pad = -(-spec // 8) * 8
    anywhere = pl.BlockSpec(memory_space=pl.ANY)
    vmem = pl.BlockSpec(memory_space=pltpu.VMEM)
    held = pl.pallas_call(
        functools.partial(kernel, (spec, nx, ny, nz, nclass)),
        out_shape=pltpu.VMEM((nx, ny, pad, nz), F32),
        in_specs=[anywhere] * 7,
        out_specs=vmem,
        scratch_shapes=[
            pltpu.VMEM((nx + 2, ny + 2, pad, nz), F32),
            pltpu.VMEM((nx + 2, ny + 2, pad, nz), F32),
            pltpu.VMEM((SPAN, pad, 2 * nz), F32),
            pltpu.VMEM((pad, nz), F32),
            pltpu.VMEM((1, spec), F32),
            pltpu.VMEM((spec, spec), F32),
            pltpu.VMEM((spec, nclass, spec), F32),
            pltpu.VMEM((nclass * pad, 128), F32),
            pltpu.VMEM((128, 128), F32),
            pltpu.VMEM((nclass * pad, 4 * pad), BF16),
            pltpu.VMEM((nclass * pad, 4 * pad), BF16),
            pltpu.VMEM((nx * ny, nz), jnp.int32),
            pltpu.SMEM((nclass,), F32),
            pltpu.SMEM((nclass,), jnp.int32),
            pltpu.SemaphoreType.DMA((nx, ny)),
            pltpu.SemaphoreType.DMA((6,)),
            pltpu.SemaphoreType.DMA((2, 2, ny)),
            pltpu.SemaphoreType.DMA((2, 2, ny)),
            pltpu.SemaphoreType.DMA((2, 2)),
            pltpu.SemaphoreType.DMA((2, 2)),
        ],
        compiler_params=pltpu.CompilerParams(
            collective_id=0, has_side_effects=True, vmem_limit_bytes=60 * 1024 * 1024),
    )(
        species, diffusion.reshape(1, spec), class_rate,
        mixing, inverses.transpose(1, 0, 2), newton_counts, cell_class.reshape(nx * ny, nz),
    )
    return pl.pallas_call(
        deliver,
        out_shape=jax.ShapeDtypeStruct(species.shape, F32),
        in_specs=[vmem],
        out_specs=anywhere,
        scratch_shapes=[pltpu.SemaphoreType.DMA((nx, ny))],
    )(pltpu.with_memory_space_constraint(held, pltpu.VMEM))


def solution(mesh):
    in_specs = (P(None, "gx", "gy", None), P(), P(), P(), P(), P(), P("gx", "gy", None))
    out_specs = P(None, "gx", "gy", None)
    return jax.shard_map(local, mesh=mesh, in_specs=in_specs, out_specs=out_specs, check_vma=False)
```

time: 30.3 us -> 26.7 us (0.88)
  the two profiles are of different devices: /device:TPU:3 before, /device:TPU:18 now
where the time goes in v1:
time: 26.7 us; the launch traced here: 26.6 us
  Pallas kernels  26.6 us (100%)
    pallas_call x1, Pallas kernels, local(): pl.pallas_call(functools.partial(kernel, (spec, nx, ny, nz, nclass)), out...  25.4 us
    pallas_call x1, Pallas kernels, local(): pl.pallas_call(deliver, out_shape=jax.ShapeDtypeStruct(species.shape, F32...  1.16 us

profile of v1, /device:TPU:18, one launch (start us, length us, event | category | flops | bytes accessed | tf_op | source)
XLA Modules:
  0.0 26.6 jit_solution(12741431497687997814)
XLA Ops:
  0.0 25.4 %shard_map.73.held = f32[4,8,56,128]{3,2,1,0:T(8,128)S(1)} custom-call(f32[53,4,8,128]{3,2,1,0:T(8,128)} %species_hbm.1, f32[1,53]{1,0:T(1,128)} %bitcast.5, f32[4]{0:T(128)} %rate_hbm.1, f32[53,53]{1,0:T(8,128)} %mixing_hbm.1, f32[53,4,53]{2,1,0:T(4,128)} %bitcast.3, s32[4]{0:T(128)} %counts_hbm.1, s32[32,128]{1,0:T(8,128)} %bitcast.4), custom_call_target="tpu_custom_call" | custom-call | tf_op jit(solution)/shard_map/pallas_call | solution.py:300
  25.4 1.2 %shard_map.74 = f32[53,4,8,128]{3,2,1,0:T(8,128)} custom-call(f32[4,8,56,128]{3,2,1,0:T(8,128)S(1)} %shard_map.73.held), custom_call_target="tpu_custom_call" | custom-call | tf_op jit(solution)/shard_map/pallas_call | solution.py:333

commit v2 on v1

--- a/solution.py
+++ b/solution.py
@@ -35,18 +35,32 @@
     to_x = ((gx - 1, gy), (gx + 1, gy))
     to_y = ((gx, gy - 1), (gx, gy + 1))
     edges = pairs_of(ny)
-
-    def load(x, y):
-        return pltpu.make_async_copy(
-            species_hbm.at[:, x, y], ext.at[x + 1, y + 1, real], load_sem.at[x, y])
+    order = [y for pair in edges for y in pair]
+    slot = {y: at + 1 for at, y in enumerate(order)} | {-1: 0, ny: ny + 1}
+    wide = len(edges[0])
+
+    def span(c):
+        return pl.ds(slot[edges[c][0]], len(edges[c]))
 
     sides = sorted({0, nx - 1})
-    first = [(x, y) for y in edges[0] for x in sides]
-    first += [(x, y) for y in edges[0] for x in range(1, nx - 1)]
-    first += [(x, y) for pair in edges[1:] for y in pair for x in sides]
-    later = [(x, y) for pair in edges[1:] for y in pair for x in range(1, nx - 1)]
-    for x, y in first + later:
-        load(x, y).start()
+    middle = list(range(1, nx - 1))
+    free = [(x, y) for y in order[wide:] for x in middle]
+    rim = [(x, y) for y in order[:wide] for x in middle]
+    face = [(x, y) for y in order for x in sides]
+    corner = wide * len(sides)
+    groups = [([(x, y) for y in order], (pl.ds(x + 1, 1), pl.ds(1, ny))) for x in sides]
+    groups += [(rim, (pl.ds(2, nx - 2), pl.ds(1, wide))), (free, (pl.ds(2, nx - 2), pl.ds(1 + wide, ny - wide)))]
+    groups = [group for group in groups if group[0]]
+    kind = {cell: i for i, (cells, _) in enumerate(groups) for cell in cells}
+    for x, y in face[:corner] + rim + face[corner:] + free:
+        pltpu.make_async_copy(
+            species_hbm.at[:, x, y], ext.at[x + 1, slot[y], real], load_sem.at[kind[x, y]]).start()
+
+    def loaded(i):
+        box = groups[i][1]
+        pltpu.make_async_copy(
+            ext2.at[box[0], box[1], real], ext.at[box[0], box[1], real], load_sem.at[i]).wait()
+
     small = [
         pltpu.make_async_copy(src, dst, small_sem.at[i]) for i, (src, dst) in enumerate((
             (mixing_hbm, mix), (inverses_hbm, inv), (diffusion_hbm, row),
@@ -75,43 +89,50 @@
         def _():
             for buf in (ext, ext2):
                 for y in range(ny):
-                    buf[side * (nx + 1), y + 1, real] = blank
+                    buf[side * (nx + 1), slot[y], real] = blank
         @pl.when(jnp.logical_not(has_y[side]))
         def _():
             for buf in (ext, ext2):
                 for x in range(nx):
                     buf[x + 1, side * (ny + 1), real] = blank
 
-    def x_copy(stage, side, y):
+    def x_copy(stage, side, c):
         buf = (ext, ext2)[stage]
         src_row, dst_row = (1, nx + 1) if side == 0 else (nx, 0)
         return pltpu.make_async_remote_copy(
-            src_ref=buf.at[src_row, y + 1, real], dst_ref=buf.at[dst_row, y + 1, real],
-            send_sem=xs_send.at[stage, side, y], recv_sem=xs_recv.at[stage, side, y],
+            src_ref=buf.at[src_row, span(c), real], dst_ref=buf.at[dst_row, span(c), real],
+            send_sem=xs_send.at[stage, side], recv_sem=xs_recv.at[stage, side, c],
             device_id=to_x[side], device_id_type=MESH)
+
+    def x_face(stage, side):
+        buf = (ext, ext2)[stage]
+        rows = buf.at[1 if side == 0 else nx, pl.ds(1, ny), real]
+        return pltpu.make_async_remote_copy(
+            src_ref=rows, dst_ref=rows, send_sem=xs_send.at[stage, side],
+            recv_sem=xs_recv.at[stage, side, 0], device_id=to_x[side], device_id_type=MESH)
 
     def y_copy(stage, side):
         buf = (ext, ext2)[stage]
-        src_col, dst_col = (1, ny + 1) if side == 0 else (ny, 0)
+        src_col, dst_col = (slot[0], ny + 1) if side == 0 else (slot[ny - 1], 0)
         return pltpu.make_async_remote_copy(
             src_ref=buf.at[pl.ds(1, nx), src_col, real],
             dst_ref=buf.at[pl.ds(1, nx), dst_col, real],
             send_sem=ys_send.at[stage, side], recv_sem=ys_recv.at[stage, side],
             device_id=to_y[side], device_id_type=MESH)
 
-    def x_start(stage, ys):
+    def x_start(stage, cs):
         for side in (0, 1):
             @pl.when(has_x[side])
             def _():
-                for y in ys:
-                    x_copy(stage, side, y).start()
-
-    def x_arrive(stage, ys):
+                for c in cs:
+                    x_copy(stage, side, c).start()
+
+    def x_arrive(stage, cs):
         for side in (0, 1):
             @pl.when(has_x[side])
             def _():
-                for y in ys:
-                    x_copy(stage, 1 - side, y).wait_recv()
+                for c in cs:
+                    x_copy(stage, 1 - side, c).wait_recv()
 
     def y_start(stage):
         for side in (0, 1):
@@ -127,12 +148,13 @@
 
     neighbours = sum(has.astype(jnp.int32) for has in has_x + has_y)
     pl.semaphore_wait(barrier, neighbours)
-    for x, y in first:
-        load(x, y).wait()
-    x_start(0, edges[0])
+    for i in range(len(groups) - bool(free)):
+        loaded(i)
+    per = max(1, SPAN // 2)
+    batches = [range(len(edges))[c:c + per] for c in range(0, len(edges), per)]
+    x_start(0, batches[0][:1])
     y_start(0)
-    for pair in edges[1:]:
-        x_start(0, pair)
+    x_start(0, batches[0][1:])
 
     for copy in small:
         copy.wait()
@@ -169,8 +191,9 @@
     lane = lax.broadcasted_iota(jnp.int32, (pad, nz), 1)
 
     def laplace(buf, x, y):
-        v = buf[x + 1, y + 1]
-        total = buf[x + 2, y + 1] + buf[x, y + 1] + buf[x + 1, y + 2] + buf[x + 1, y]
+        at = slot[y]
+        v = buf[x + 1, at]
+        total = buf[x + 2, at] + buf[x, at] + buf[x + 1, slot[y + 1]] + buf[x + 1, slot[y - 1]]
         total = total + jnp.where(lane == nz - 1, 0.0, pltpu.roll(v, nz - 1, 1))
         total = total + jnp.where(lane == 0, 0.0, pltpu.roll(v, 1, 1))
         return v, total - 6.0 * v
@@ -226,7 +249,7 @@
         for g, (cells, state) in enumerate(zip(groups, states)):
             end = value(g, state)
             for i, (x, y) in enumerate(cells):
-                ext2[x + 1, y + 1] = end[:, i * nz:(i + 1) * nz]
+                ext2[x + 1, slot[y]] = end[:, i * nz:(i + 1) * nz]
 
     def pack(cells):
         return [cells[i:i + 2] for i in range(0, len(cells), 2)]
@@ -236,22 +259,19 @@
         for i in range(0, len(groups), SPAN):
             solve(groups[i:i + SPAN])
 
-    for x, y in later:
-        load(x, y).wait()
-    middle = list(range(1, nx - 1))
-    free = [(x, y) for pair in edges[1:] for y in pair for x in middle]
-    rim = [(x, y) for y in edges[0] for x in middle]
+    if free:
+        loaded(len(groups) - 1)
     now = 2 * SPAN * (len(free) // (2 * SPAN))
     solve_all(free[:now])
+    for batch in batches[1:]:
+        x_start(0, batch)
     y_arrive(0)
     solve_all(free[now:] + rim)
-    per = max(1, SPAN // 2)
-    for c in range(0, len(edges), per):
-        ys = [y for pair in edges[c:c + per] for y in pair]
-        x_arrive(0, ys)
-        solve_all([(x, y) for y in ys for x in sides])
-        x_start(1, ys)
-        if c == 0:
+    for i, batch in enumerate(batches):
+        x_arrive(0, batch)
+        solve_all([(x, y) for c in batch for y in edges[c] for x in sides])
+        x_start(1, batch)
+        if i == 0:
             y_start(1)
 
     def finish(x, y):
@@ -263,8 +283,8 @@
     y_arrive(1)
     for x, y in rim:
         finish(x, y)
-    for pair in edges:
-        x_arrive(1, pair)
+    for c, pair in enumerate(edges):
+        x_arrive(1, [c])
         for y in pair:
             for x in sides:
                 finish(x, y)
@@ -273,8 +293,7 @@
         for side in (0, 1):
             @pl.when(has_x[side])
             def _():
-                for y in range(ny):
-                    x_copy(stage, side, y).wait_send()
+                x_face(stage, side).wait_send()
             @pl.when(has_y[side])
             def _():
                 y_copy(stage, side).wait_send()
@@ -283,12 +302,12 @@
 def deliver(held, out_hbm, sem):
     spec, nx, ny, _ = out_hbm.shape
     copies = [
-        pltpu.make_async_copy(held.at[x, y, pl.ds(0, spec)], out_hbm.at[:, x, y], sem.at[x, y])
+        pltpu.make_async_copy(held.at[x, y, pl.ds(0, spec)], out_hbm.at[:, x, y], sem)
         for x in range(nx) for y in range(ny)]
     for copy in copies:
         copy.start()
-    for copy in copies:
-        copy.wait()
+    every = held.at[:, :, pl.ds(0, spec)]
+    pltpu.make_async_copy(every, every, sem).wait()
 
 
 def local(species, diffusion, class_rate, mixing, inverses, newton_counts, cell_class):
@@ -317,10 +336,10 @@
             pltpu.VMEM((nx * ny, nz), jnp.int32),
             pltpu.SMEM((nclass,), F32),
             pltpu.SMEM((nclass,), jnp.int32),
-            pltpu.SemaphoreType.DMA((nx, ny)),
+            pltpu.SemaphoreType.DMA((4,)),
             pltpu.SemaphoreType.DMA((6,)),
-            pltpu.SemaphoreType.DMA((2, 2, ny)),
-            pltpu.SemaphoreType.DMA((2, 2, ny)),
+            pltpu.SemaphoreType.DMA((2, 2)),
+            pltpu.SemaphoreType.DMA((2, 2, (ny + 1) // 2)),
             pltpu.SemaphoreType.DMA((2, 2)),
             pltpu.SemaphoreType.DMA((2, 2)),
         ],
@@ -335,7 +354,7 @@
         out_shape=jax.ShapeDtypeStruct(species.shape, F32),
         in_specs=[vmem],
         out_specs=anywhere,
-        scratch_shapes=[pltpu.SemaphoreType.DMA((nx, ny))],
+        scratch_shapes=[pltpu.SemaphoreType.DMA(())],
     )(pltpu.with_memory_space_constraint(held, pltpu.VMEM))
 
 

time: 26.7 us -> 25.7 us (0.963)
  Pallas kernels: 26.6 us -> 25.6 us
    pallas_call x1, Pallas kernels: 25.4 us -> 24.7 us  [local(): pl.pallas_call(functools.partial(kernel, (spec, nx, ny, nz, nclass)), out...]
    pallas_call x1, Pallas kernels: 1.16 us -> 0.88 us  [local(): pl.pallas_call(deliver, out_shape=jax.ShapeDtypeStruct(species.shape, F32...]
where the time goes in v2:
time: 25.7 us; the launch traced here: 25.6 us
  Pallas kernels  25.6 us (100%)
    pallas_call x1, Pallas kernels, local(): pl.pallas_call(functools.partial(kernel, (spec, nx, ny, nz, nclass)), out...  24.7 us
    pallas_call x1, Pallas kernels, local(): pl.pallas_call(deliver, out_shape=jax.ShapeDtypeStruct(species.shape, F32...  0.88 us

profile of v2, /device:TPU:18, one launch (start us, length us, event | category | flops | bytes accessed | tf_op | source)
XLA Modules:
  0.0 25.6 jit_solution(9242841329019179797)
XLA Ops:
  0.0 24.7 %shard_map.73.held = f32[4,8,56,128]{3,2,1,0:T(8,128)S(1)} custom-call(f32[53,4,8,128]{3,2,1,0:T(8,128)} %species_hbm.1, f32[1,53]{1,0:T(1,128)} %bitcast.5, f32[4]{0:T(128)} %rate_hbm.1, f32[53,53]{1,0:T(8,128)} %mixing_hbm.1, f32[53,4,53]{2,1,0:T(4,128)} %bitcast.3, s32[4]{0:T(128)} %counts_hbm.1, s32[32,128]{1,0:T(8,128)} %bitcast.4), custom_call_target="tpu_custom_call" | custom-call | tf_op jit(solution)/shard_map/pallas_call | solution.py:319
  24.7 0.9 %shard_map.74 = f32[53,4,8,128]{3,2,1,0:T(8,128)} custom-call(f32[4,8,56,128]{3,2,1,0:T(8,128)S(1)} %shard_map.73.held), custom_call_target="tpu_custom_call" | custom-call | tf_op jit(solution)/shard_map/pallas_call | solution.py:352

commit v3 on v2

--- a/solution.py
+++ b/solution.py
@@ -8,7 +8,8 @@
 from jax.sharding import PartitionSpec as P
 
 NMAX = 8
-SPAN = 4
+SPAN = 6
+WHEN = 3
 MESH = pl.DeviceIdType.MESH
 F32 = jnp.float32
 BF16 = jnp.bfloat16
@@ -39,9 +40,7 @@
     slot = {y: at + 1 for at, y in enumerate(order)} | {-1: 0, ny: ny + 1}
     wide = len(edges[0])
 
-    def span(c):
-        return pl.ds(slot[edges[c][0]], len(edges[c]))
-
+    pieces = ([pl.ds(1, ny)], [pl.ds(slot[pair[0]], len(pair)) for pair in edges])
     sides = sorted({0, nx - 1})
     middle = list(range(1, nx - 1))
     free = [(x, y) for y in order[wide:] for x in middle]
@@ -100,8 +99,9 @@
         buf = (ext, ext2)[stage]
         src_row, dst_row = (1, nx + 1) if side == 0 else (nx, 0)
         return pltpu.make_async_remote_copy(
-            src_ref=buf.at[src_row, span(c), real], dst_ref=buf.at[dst_row, span(c), real],
-            send_sem=xs_send.at[stage, side], recv_sem=xs_recv.at[stage, side, c],
+            src_ref=buf.at[src_row, pieces[stage][c], real],
+            dst_ref=buf.at[dst_row, pieces[stage][c], real],
+            send_sem=xs_send.at[stage, side], recv_sem=xs_recv.at[side, stage + c],
             device_id=to_x[side], device_id_type=MESH)
 
     def x_face(stage, side):
@@ -109,7 +109,7 @@
         rows = buf.at[1 if side == 0 else nx, pl.ds(1, ny), real]
         return pltpu.make_async_remote_copy(
             src_ref=rows, dst_ref=rows, send_sem=xs_send.at[stage, side],
-            recv_sem=xs_recv.at[stage, side, 0], device_id=to_x[side], device_id_type=MESH)
+            recv_sem=xs_recv.at[side, 0], device_id=to_x[side], device_id_type=MESH)
 
     def y_copy(stage, side):
         buf = (ext, ext2)[stage]
@@ -120,19 +120,26 @@
             send_sem=ys_send.at[stage, side], recv_sem=ys_recv.at[stage, side],
             device_id=to_y[side], device_id_type=MESH)
 
-    def x_start(stage, cs):
+    even = gx % 2 == 0
+    near = (jnp.logical_not(even), even)
+
+    def facing(close):
         for side in (0, 1):
-            @pl.when(has_x[side])
-            def _():
-                for c in cs:
+            mine = near[side] if close else jnp.logical_not(near[side])
+            yield side, jnp.logical_and(has_x[side], mine)
+
+    def x_start(stage, close):
+        for side, there in facing(close):
+            @pl.when(there)
+            def _():
+                for c in range(len(pieces[stage])):
                     x_copy(stage, side, c).start()
 
-    def x_arrive(stage, cs):
-        for side in (0, 1):
-            @pl.when(has_x[side])
-            def _():
-                for c in cs:
-                    x_copy(stage, 1 - side, c).wait_recv()
+    def x_arrive(stage, close, c):
+        for side, there in facing(close):
+            @pl.when(there)
+            def _():
+                x_copy(stage, 1 - side, c).wait_recv()
 
     def y_start(stage):
         for side in (0, 1):
@@ -150,11 +157,8 @@
     pl.semaphore_wait(barrier, neighbours)
     for i in range(len(groups) - bool(free)):
         loaded(i)
-    per = max(1, SPAN // 2)
-    batches = [range(len(edges))[c:c + per] for c in range(0, len(edges), per)]
-    x_start(0, batches[0][:1])
+    x_start(0, True)
     y_start(0)
-    x_start(0, batches[0][1:])
 
     for copy in small:
         copy.wait()
@@ -198,7 +202,7 @@
         total = total + jnp.where(lane == 0, 0.0, pltpu.roll(v, 1, 1))
         return v, total - 6.0 * v
 
-    def solve(groups):
+    def solve(groups, hook):
         states, shrinks, whiches, limits = [], [], [], []
         for g, cells in enumerate(groups):
             parts = []
@@ -245,7 +249,11 @@
                 result.append(state + jnp.concatenate(tiles, axis=0))
             return tuple(result)
 
-        states = lax.fori_loop(0, NMAX, step, tuple(states), unroll=NMAX)
+        states, part = tuple(states), NMAX if hook is None else WHEN
+        states = lax.fori_loop(0, part, step, states, unroll=part)
+        if hook is not None:
+            hook()
+            states = lax.fori_loop(part, NMAX, step, states, unroll=NMAX - part)
         for g, (cells, state) in enumerate(zip(groups, states)):
             end = value(g, state)
             for i, (x, y) in enumerate(cells):
@@ -254,25 +262,25 @@
     def pack(cells):
         return [cells[i:i + 2] for i in range(0, len(cells), 2)]
 
-    def solve_all(cells):
+    def solve_all(cells, hook=None):
         groups = pack(cells)
         for i in range(0, len(groups), SPAN):
-            solve(groups[i:i + SPAN])
+            solve(groups[i:i + SPAN], hook if i == 0 else None)
 
     if free:
         loaded(len(groups) - 1)
-    now = 2 * SPAN * (len(free) // (2 * SPAN))
-    solve_all(free[:now])
-    for batch in batches[1:]:
-        x_start(0, batch)
+    near_x = (1 - gx % 2) * (nx - 1)
+    far_x = nx - 1 - near_x
+    solve_all(free)
     y_arrive(0)
-    solve_all(free[now:] + rim)
-    for i, batch in enumerate(batches):
-        x_arrive(0, batch)
-        solve_all([(x, y) for c in batch for y in edges[c] for x in sides])
-        x_start(1, batch)
-        if i == 0:
-            y_start(1)
+    solve_all(rim, lambda: x_start(0, False))
+    x_arrive(0, True, 0)
+    solve_all([(near_x, y) for y in order])
+    x_start(1, True)
+    x_arrive(0, False, 0)
+    solve_all([(far_x, y) for y in order])
+    x_start(1, False)
+    y_start(1)
 
     def finish(x, y):
         v, lap = laplace(ext2, x, y)
@@ -283,17 +291,19 @@
     y_arrive(1)
     for x, y in rim:
         finish(x, y)
-    for c, pair in enumerate(edges):
-        x_arrive(1, [c])
-        for y in pair:
-            for x in sides:
+    for close, x in ((True, near_x), (False, far_x)):
+        for c, pair in enumerate(edges):
+            x_arrive(1, close, c)
+            for y in pair:
                 finish(x, y)
 
     for stage in (0, 1):
+        for close in (True, False):
+            for side, there in facing(close):
+                @pl.when(there)
+                def _():
+                    x_face(stage, side).wait_send()
         for side in (0, 1):
-            @pl.when(has_x[side])
-            def _():
-                x_face(stage, side).wait_send()
             @pl.when(has_y[side])
             def _():
                 y_copy(stage, side).wait_send()
@@ -339,7 +349,7 @@
             pltpu.SemaphoreType.DMA((4,)),
             pltpu.SemaphoreType.DMA((6,)),
             pltpu.SemaphoreType.DMA((2, 2)),
-            pltpu.SemaphoreType.DMA((2, 2, (ny + 1) // 2)),
+            pltpu.SemaphoreType.DMA((2, 1 + (ny + 1) // 2)),
             pltpu.SemaphoreType.DMA((2, 2)),
             pltpu.SemaphoreType.DMA((2, 2)),
         ],

time: 25.7 us -> 24.6 us (0.957)
  the two profiles are of different devices: /device:TPU:18 before, /device:TPU:10 now
where the time goes in v3:
time: 24.6 us; the launch traced here: 24.5 us
  Pallas kernels  24.5 us (100%)
    pallas_call x1, Pallas kernels, local(): pl.pallas_call(functools.partial(kernel, (spec, nx, ny, nz, nclass)), out...  23.6 us
    pallas_call x1, Pallas kernels, local(): pl.pallas_call(deliver, out_shape=jax.ShapeDtypeStruct(species.shape, F32...  0.88 us

profile of v3, /device:TPU:10, one launch (start us, length us, event | category | flops | bytes accessed | tf_op | source)
XLA Modules:
  0.0 24.5 jit_solution(10625051632615928820)
XLA Ops:
  0.0 23.6 %shard_map.73.held = f32[4,8,56,128]{3,2,1,0:T(8,128)S(1)} custom-call(f32[53,4,8,128]{3,2,1,0:T(8,128)} %species_hbm.1, f32[1,53]{1,0:T(1,128)} %bitcast.5, f32[4]{0:T(128)} %rate_hbm.1, f32[53,53]{1,0:T(8,128)} %mixing_hbm.1, f32[53,4,53]{2,1,0:T(4,128)} %bitcast.3, s32[4]{0:T(128)} %counts_hbm.1, s32[32,128]{1,0:T(8,128)} %bitcast.4), custom_call_target="tpu_custom_call" | custom-call | tf_op jit(solution)/shard_map/pallas_call | solution.py:329
  23.6 0.9 %shard_map.74 = f32[53,4,8,128]{3,2,1,0:T(8,128)} custom-call(f32[4,8,56,128]{3,2,1,0:T(8,128)S(1)} %shard_map.73.held), custom_call_target="tpu_custom_call" | custom-call | tf_op jit(solution)/shard_map/pallas_call | solution.py:362

commit v4 on v3

--- a/solution.py
+++ b/solution.py
@@ -8,8 +8,7 @@
 from jax.sharding import PartitionSpec as P
 
 NMAX = 8
-SPAN = 6
-WHEN = 3
+SPAN = 4
 MESH = pl.DeviceIdType.MESH
 F32 = jnp.float32
 BF16 = jnp.bfloat16
@@ -35,12 +34,21 @@
     has_y = (gy > 0, gy < sy - 1)
     to_x = ((gx - 1, gy), (gx + 1, gy))
     to_y = ((gx, gy - 1), (gx, gy + 1))
+    barrier = pltpu.get_barrier_semaphore()
+    for has, to in zip(has_x + has_y, to_x + to_y):
+        @pl.when(has)
+        def _():
+            pl.semaphore_signal(barrier, inc=1, device_id=to, device_id_type=MESH)
+
     edges = pairs_of(ny)
     order = [y for pair in edges for y in pair]
     slot = {y: at + 1 for at, y in enumerate(order)} | {-1: 0, ny: ny + 1}
     wide = len(edges[0])
 
-    pieces = ([pl.ds(1, ny)], [pl.ds(slot[pair[0]], len(pair)) for pair in edges])
+    cut = (len(edges) + 1) // 2
+    halves = [edges[:cut], edges[cut:]] if edges[cut:] else [edges]
+    columns = [[y for pair in half for y in pair] for half in halves]
+    pieces = [pl.ds(slot[half[0]], len(half)) for half in columns]
     sides = sorted({0, nx - 1})
     middle = list(range(1, nx - 1))
     free = [(x, y) for y in order[wide:] for x in middle]
@@ -66,12 +74,6 @@
             (rate_hbm, rates), (counts_hbm, counts), (class_hbm, classes)))]
     for copy in small:
         copy.start()
-
-    barrier = pltpu.get_barrier_semaphore()
-    for has, to in zip(has_x + has_y, to_x + to_y):
-        @pl.when(has)
-        def _():
-            pl.semaphore_signal(barrier, inc=1, device_id=to, device_id_type=MESH)
 
     tail = jnp.zeros((pad - spec, nz), F32)
     for x in range(nx + 2):
@@ -99,9 +101,9 @@
         buf = (ext, ext2)[stage]
         src_row, dst_row = (1, nx + 1) if side == 0 else (nx, 0)
         return pltpu.make_async_remote_copy(
-            src_ref=buf.at[src_row, pieces[stage][c], real],
-            dst_ref=buf.at[dst_row, pieces[stage][c], real],
-            send_sem=xs_send.at[stage, side], recv_sem=xs_recv.at[side, stage + c],
+            src_ref=buf.at[src_row, pieces[c], real],
+            dst_ref=buf.at[dst_row, pieces[c], real],
+            send_sem=xs_send.at[stage, side], recv_sem=xs_recv.at[side, stage * len(halves) + c],
             device_id=to_x[side], device_id_type=MESH)
 
     def x_face(stage, side):
@@ -128,11 +130,11 @@
             mine = near[side] if close else jnp.logical_not(near[side])
             yield side, jnp.logical_and(has_x[side], mine)
 
-    def x_start(stage, close):
+    def x_start(stage, close, cs=None):
         for side, there in facing(close):
             @pl.when(there)
             def _():
-                for c in range(len(pieces[stage])):
+                for c in range(len(pieces)) if cs is None else cs:
                     x_copy(stage, side, c).start()
 
     def x_arrive(stage, close, c):
@@ -202,7 +204,7 @@
         total = total + jnp.where(lane == 0, 0.0, pltpu.roll(v, 1, 1))
         return v, total - 6.0 * v
 
-    def solve(groups, hook):
+    def solve(groups):
         states, shrinks, whiches, limits = [], [], [], []
         for g, cells in enumerate(groups):
             parts = []
@@ -249,11 +251,7 @@
                 result.append(state + jnp.concatenate(tiles, axis=0))
             return tuple(result)
 
-        states, part = tuple(states), NMAX if hook is None else WHEN
-        states = lax.fori_loop(0, part, step, states, unroll=part)
-        if hook is not None:
-            hook()
-            states = lax.fori_loop(part, NMAX, step, states, unroll=NMAX - part)
+        states = lax.fori_loop(0, NMAX, step, tuple(states), unroll=NMAX)
         for g, (cells, state) in enumerate(zip(groups, states)):
             end = value(g, state)
             for i, (x, y) in enumerate(cells):
@@ -262,40 +260,64 @@
     def pack(cells):
         return [cells[i:i + 2] for i in range(0, len(cells), 2)]
 
-    def solve_all(cells, hook=None):
+    def solve_all(cells):
         groups = pack(cells)
         for i in range(0, len(groups), SPAN):
-            solve(groups[i:i + SPAN], hook if i == 0 else None)
+            solve(groups[i:i + SPAN])
 
     if free:
         loaded(len(groups) - 1)
     near_x = (1 - gx % 2) * (nx - 1)
     far_x = nx - 1 - near_x
-    solve_all(free)
+    first = 2 * (2 * len(free) // 6)
+    solve_all(free[:first])
+    solve_all(free[first:])
+    x_start(0, False, [0])
     y_arrive(0)
-    solve_all(rim, lambda: x_start(0, False))
-    x_arrive(0, True, 0)
+    for h in range(len(halves)):
+        x_arrive(0, True, h)
+    x_start(0, False, range(1, len(halves)))
     solve_all([(near_x, y) for y in order])
     x_start(1, True)
-    x_arrive(0, False, 0)
-    solve_all([(far_x, y) for y in order])
-    x_start(1, False)
+    for h, half in enumerate(columns):
+        x_arrive(0, False, h)
+        last = h == len(halves) - 1
+        solve_all([(far_x, y) for y in half] + (rim if last else []))
+        x_start(1, False, [h])
     y_start(1)
 
     def finish(x, y):
         v, lap = laplace(ext2, x, y)
         out[x, y] = v + 0.5 * (coef[...] * lap - out[x, y])
 
+    def inside(x, y):
+        at = slot[y]
+        v = ext2[x + 1, at]
+        total = ext2[jnp.where(x == 0, 2, nx - 1), at]
+        total = total + ext2[x + 1, slot[y + 1]] + ext2[x + 1, slot[y - 1]]
+        total = total + jnp.where(lane == nz - 1, 0.0, pltpu.roll(v, nz - 1, 1))
+        total = total + jnp.where(lane == 0, 0.0, pltpu.roll(v, 1, 1))
+        out[x, y] = v + 0.5 * (coef[...] * (total - 6.0 * v) - out[x, y])
+
+    def across(x, y):
+        out[x, y] = out[x, y] + 0.5 * coef[...] * ext2[jnp.where(x == 0, 0, nx + 1), slot[y]]
+
     for x, y in free:
         finish(x, y)
+    for y in order[wide:]:
+        for x in (near_x, far_x):
+            inside(x, y)
     y_arrive(1)
     for x, y in rim:
         finish(x, y)
-    for close, x in ((True, near_x), (False, far_x)):
-        for c, pair in enumerate(edges):
-            x_arrive(1, close, c)
-            for y in pair:
-                finish(x, y)
+    for y in order[:wide]:
+        for x in (near_x, far_x):
+            inside(x, y)
+    for close, x in ((False, far_x), (True, near_x)):
+        for h, half in enumerate(columns):
+            x_arrive(1, close, h)
+            for y in half:
+                across(x, y)
 
     for stage in (0, 1):
         for close in (True, False):
@@ -349,7 +371,7 @@
             pltpu.SemaphoreType.DMA((4,)),
             pltpu.SemaphoreType.DMA((6,)),
             pltpu.SemaphoreType.DMA((2, 2)),
-            pltpu.SemaphoreType.DMA((2, 1 + (ny + 1) // 2)),
+            pltpu.SemaphoreType.DMA((2, 4)),
             pltpu.SemaphoreType.DMA((2, 2)),
             pltpu.SemaphoreType.DMA((2, 2)),
         ],

time: 24.6 us -> 24.8 us (level)
  the two profiles are of different devices: /device:TPU:10 before, /device:TPU:3 now
where the time goes in v4:
time: 24.8 us; the launch traced here: 24.3 us
  Pallas kernels  24.3 us (98%)
    pallas_call x1, Pallas kernels, local(): pl.pallas_call(functools.partial(kernel, (spec, nx, ny, nz, nclass)), out...  23.4 us
    pallas_call x1, Pallas kernels, local(): pl.pallas_call(deliver, out_shape=jax.ShapeDtypeStruct(species.shape, F32...  0.88 us

profile of v4, /device:TPU:3, one launch (start us, length us, event | category | flops | bytes accessed | tf_op | source)
XLA Modules:
  0.0 24.3 jit_solution(17573420722571072466)
XLA Ops:
  0.0 23.4 %shard_map.73.held = f32[4,8,56,128]{3,2,1,0:T(8,128)S(1)} custom-call(f32[53,4,8,128]{3,2,1,0:T(8,128)} %species_hbm.1, f32[1,53]{1,0:T(1,128)} %bitcast.5, f32[4]{0:T(128)} %rate_hbm.1, f32[53,53]{1,0:T(8,128)} %mixing_hbm.1, f32[53,4,53]{2,1,0:T(4,128)} %bitcast.3, s32[4]{0:T(128)} %counts_hbm.1, s32[32,128]{1,0:T(8,128)} %bitcast.4), custom_call_target="tpu_custom_call" | custom-call | tf_op jit(solution)/shard_map/pallas_call | solution.py:351
  23.5 0.9 %shard_map.74 = f32[53,4,8,128]{3,2,1,0:T(8,128)} custom-call(f32[4,8,56,128]{3,2,1,0:T(8,128)S(1)} %shard_map.73.held), custom_call_target="tpu_custom_call" | custom-call | tf_op jit(solution)/shard_map/pallas_call | solution.py:384

commit v5 on v4

--- a/solution.py
+++ b/solution.py
@@ -204,7 +204,7 @@
         total = total + jnp.where(lane == 0, 0.0, pltpu.roll(v, 1, 1))
         return v, total - 6.0 * v
 
-    def solve(groups):
+    def solve(groups, hook):
         states, shrinks, whiches, limits = [], [], [], []
         for g, cells in enumerate(groups):
             parts = []
@@ -251,7 +251,11 @@
                 result.append(state + jnp.concatenate(tiles, axis=0))
             return tuple(result)
 
-        states = lax.fori_loop(0, NMAX, step, tuple(states), unroll=NMAX)
+        part = NMAX if hook is None else NMAX - 1
+        states = lax.fori_loop(0, part, step, tuple(states), unroll=part)
+        if hook is not None:
+            hook()
+            states = step(part, states)
         for g, (cells, state) in enumerate(zip(groups, states)):
             end = value(g, state)
             for i, (x, y) in enumerate(cells):
@@ -260,10 +264,12 @@
     def pack(cells):
         return [cells[i:i + 2] for i in range(0, len(cells), 2)]
 
-    def solve_all(cells):
+    def solve_all(cells, hook=None):
         groups = pack(cells)
         for i in range(0, len(groups), SPAN):
-            solve(groups[i:i + SPAN])
+            solve(groups[i:i + SPAN], hook)
+        if hook is not None and not groups:
+            hook()
 
     if free:
         loaded(len(groups) - 1)
@@ -271,8 +277,7 @@
     far_x = nx - 1 - near_x
     first = 2 * (2 * len(free) // 6)
     solve_all(free[:first])
-    solve_all(free[first:])
-    x_start(0, False, [0])
+    solve_all(free[first:], lambda: x_start(0, False, [0]))
     y_arrive(0)
     for h in range(len(halves)):
         x_arrive(0, True, h)

time: 24.8 us -> 24.5 us (0.988)
    pallas_call x1, Pallas kernels: 23.4 us -> 23.2 us  [local(): pl.pallas_call(functools.partial(kernel, (spec, nx, ny, nz, nclass)), out...]
where the time goes in v5:
time: 24.5 us; the launch traced here: 24.1 us
  Pallas kernels  24.1 us (98%)
    pallas_call x1, Pallas kernels, local(): pl.pallas_call(functools.partial(kernel, (spec, nx, ny, nz, nclass)), out...  23.2 us
    pallas_call x1, Pallas kernels, local(): pl.pallas_call(deliver, out_shape=jax.ShapeDtypeStruct(species.shape, F32...  0.88 us

profile of v5, /device:TPU:3, one launch (start us, length us, event | category | flops | bytes accessed | tf_op | source)
XLA Modules:
  0.0 24.1 jit_solution(5818171313080889933)
XLA Ops:
  0.0 23.2 %shard_map.73.held = f32[4,8,56,128]{3,2,1,0:T(8,128)S(1)} custom-call(f32[53,4,8,128]{3,2,1,0:T(8,128)} %species_hbm.1, f32[1,53]{1,0:T(1,128)} %bitcast.5, f32[4]{0:T(128)} %rate_hbm.1, f32[53,53]{1,0:T(8,128)} %mixing_hbm.1, f32[53,4,53]{2,1,0:T(4,128)} %bitcast.3, s32[4]{0:T(128)} %counts_hbm.1, s32[32,128]{1,0:T(8,128)} %bitcast.4), custom_call_target="tpu_custom_call" | custom-call | tf_op jit(solution)/shard_map/pallas_call | solution.py:356
  23.2 0.9 %shard_map.74 = f32[53,4,8,128]{3,2,1,0:T(8,128)} custom-call(f32[4,8,56,128]{3,2,1,0:T(8,128)S(1)} %shard_map.73.held), custom_call_target="tpu_custom_call" | custom-call | tf_op jit(solution)/shard_map/pallas_call | solution.py:389

commit v6 on v5

--- a/solution.py
+++ b/solution.py
@@ -103,14 +103,14 @@
         return pltpu.make_async_remote_copy(
             src_ref=buf.at[src_row, pieces[c], real],
             dst_ref=buf.at[dst_row, pieces[c], real],
-            send_sem=xs_send.at[stage, side], recv_sem=xs_recv.at[side, stage * len(halves) + c],
+            send_sem=xs_send.at[side], recv_sem=xs_recv.at[side, stage * len(halves) + c],
             device_id=to_x[side], device_id_type=MESH)
 
     def x_face(stage, side):
         buf = (ext, ext2)[stage]
         rows = buf.at[1 if side == 0 else nx, pl.ds(1, ny), real]
         return pltpu.make_async_remote_copy(
-            src_ref=rows, dst_ref=rows, send_sem=xs_send.at[stage, side],
+            src_ref=rows, dst_ref=rows, send_sem=xs_send.at[side],
             recv_sem=xs_recv.at[side, 0], device_id=to_x[side], device_id_type=MESH)
 
     def y_copy(stage, side):
@@ -119,7 +119,7 @@
         return pltpu.make_async_remote_copy(
             src_ref=buf.at[pl.ds(1, nx), src_col, real],
             dst_ref=buf.at[pl.ds(1, nx), dst_col, real],
-            send_sem=ys_send.at[stage, side], recv_sem=ys_recv.at[stage, side],
+            send_sem=ys_send.at[side], recv_sem=ys_recv.at[stage, side],
             device_id=to_y[side], device_id_type=MESH)
 
     even = gx % 2 == 0
@@ -142,6 +142,18 @@
             @pl.when(there)
             def _():
                 x_copy(stage, 1 - side, c).wait_recv()
+
+    def x_sent(stage, close):
+        for side, there in facing(close):
+            @pl.when(there)
+            def _():
+                x_face(stage, side).wait_send()
+
+    def y_sent(stage):
+        for side in (0, 1):
+            @pl.when(has_y[side])
+            def _():
+                y_copy(stage, side).wait_send()
 
     def y_start(stage):
         for side in (0, 1):
@@ -283,12 +295,16 @@
         x_arrive(0, True, h)
     x_start(0, False, range(1, len(halves)))
     solve_all([(near_x, y) for y in order])
+    x_sent(0, True)
     x_start(1, True)
     for h, half in enumerate(columns):
         x_arrive(0, False, h)
         last = h == len(halves) - 1
         solve_all([(far_x, y) for y in half] + (rim if last else []))
+        if h == 0:
+            x_sent(0, False)
         x_start(1, False, [h])
+    y_sent(0)
     y_start(1)
 
     def finish(x, y):
@@ -324,16 +340,9 @@
             for y in half:
                 across(x, y)
 
-    for stage in (0, 1):
-        for close in (True, False):
-            for side, there in facing(close):
-                @pl.when(there)
-                def _():
-                    x_face(stage, side).wait_send()
-        for side in (0, 1):
-            @pl.when(has_y[side])
-            def _():
-                y_copy(stage, side).wait_send()
+    x_sent(1, True)
+    x_sent(1, False)
+    y_sent(1)
 
 
 def deliver(held, out_hbm, sem):
@@ -375,9 +384,9 @@
             pltpu.SMEM((nclass,), jnp.int32),
             pltpu.SemaphoreType.DMA((4,)),
             pltpu.SemaphoreType.DMA((6,)),
-            pltpu.SemaphoreType.DMA((2, 2)),
+            pltpu.SemaphoreType.DMA((2,)),
             pltpu.SemaphoreType.DMA((2, 4)),
-            pltpu.SemaphoreType.DMA((2, 2)),
+            pltpu.SemaphoreType.DMA((2,)),
             pltpu.SemaphoreType.DMA((2, 2)),
         ],
         compiler_params=pltpu.CompilerParams(

time: 24.5 us -> 24.4 us (level)
  no operation moved by 1% of the time
where the time goes in v6:
time: 24.4 us; the launch traced here: 24 us
  Pallas kernels  24 us (98%)
    pallas_call x1, Pallas kernels, local(): pl.pallas_call(functools.partial(kernel, (spec, nx, ny, nz, nclass)), out...  23.1 us
    pallas_call x1, Pallas kernels, local(): pl.pallas_call(deliver, out_shape=jax.ShapeDtypeStruct(species.shape, F32...  0.88 us

profile of v6, /device:TPU:3, one launch (start us, length us, event | category | flops | bytes accessed | tf_op | source)
XLA Modules:
  0.0 24.0 jit_solution(3895784356087553820)
XLA Ops:
  0.0 23.1 %shard_map.73.held = f32[4,8,56,128]{3,2,1,0:T(8,128)S(1)} custom-call(f32[53,4,8,128]{3,2,1,0:T(8,128)} %species_hbm.1, f32[1,53]{1,0:T(1,128)} %bitcast.5, f32[4]{0:T(128)} %rate_hbm.1, f32[53,53]{1,0:T(8,128)} %mixing_hbm.1, f32[53,4,53]{2,1,0:T(4,128)} %bitcast.3, s32[4]{0:T(128)} %counts_hbm.1, s32[32,128]{1,0:T(8,128)} %bitcast.4), custom_call_target="tpu_custom_call" | custom-call | tf_op jit(solution)/shard_map/pallas_call | solution.py:365
  23.1 0.9 %shard_map.74 = f32[53,4,8,128]{3,2,1,0:T(8,128)} custom-call(f32[4,8,56,128]{3,2,1,0:T(8,128)S(1)} %shard_map.73.held), custom_call_target="tpu_custom_call" | custom-call | tf_op jit(solution)/shard_map/pallas_call | solution.py:398
